TPU v7x, 32 devices: a whole 2x2x4 slice. The times are simulated.
32 devices in a mesh: chain: 8 (over y, x, core), lane: 4 (over z).
Axes of the slice: x: 2, y: 2, z: 4, core: 2. Of those that a mesh axis runs over, the one named last changes fastest.
Arguments:
- fiedler: float32 [16, 96, 128, 128], P(None, 'chain', 'lane'), may hold values from -6 to 6
- side_labels: int32 [96, 128, 128], P('chain', 'lane'), may hold values from 0 to 1, as said below
Outputs:
- squared_image: float32 [16, 120, 128, 128], P(None, 'chain', 'lane')
- gram_blocks: float32 [2, 16, 16], replicated
Inputs may be any that keep to these rules, and one draw needn't show every extreme that they name: `side_labels`: along every line of the first dimension (fixed second and third index) the vertices of side 0 form one run of planes [a, b) with 18 <= a <= 30 and 66 <= b <= 78; all other vertices are of side 1.
All inputs are finite; a program needn't handle non-finite values.
Results may differ from a plain program's by a relative error of at most 0.0001.
Values sent between devices are 32-bit elements; how exact they have to be, the bound alone decides.
A program may use at most 128 MiB of HBM per device.

v0:
```python
import functools

import jax
import jax.numpy as jnp
import numpy as np
from jax import lax
from jax.experimental import pallas as pl
from jax.experimental.pallas import tpu as pltpu
from jax.sharding import PartitionSpec as P

REACH = 2


def band_plan(chain_count, plane_count):
    half_count = chain_count // 2
    band_planes = plane_count + plane_count // 4
    total_planes = plane_count * chain_count
    margin_planes = (band_planes - plane_count) * half_count // 2
    own_slot = np.zeros(chain_count, np.int32)
    bounds = np.zeros((2, chain_count), np.int32)
    sides = np.zeros(chain_count, np.int32)
    transfers = []
    for target in range(chain_count):
        relative = (target - chain_count // 4) % chain_count
        side = relative // half_count
        within = relative % half_count
        first = total_planes // 4 - margin_planes + side * (total_planes // 2) + within * band_planes - REACH
        slot = (target * plane_count - first + total_planes // 2) % total_planes - total_planes // 2
        low = REACH if within == 0 else 0
        high = band_planes + (REACH if within == half_count - 1 else 2 * REACH)
        own_slot[target], sides[target] = slot, side
        bounds[:, target] = low, high
        below, above = max(0, slot - low), max(0, high - slot - plane_count)
        assert below <= plane_count and above <= plane_count
        if below:
            transfers.append((below, (target - 1) % chain_count, target, 1))
        if above:
            transfers.append((above, (target + 1) % chain_count, target, 2))
    groups = []
    for count, source, target, way in sorted(transfers, reverse=True):
        for group in groups:
            if group["count"] == count and source not in group["sources"] and target not in group["targets"]:
                break
        else:
            group = dict(count=count, sources=[], targets=[], start=np.zeros(chain_count, np.int32),
                         arrives=np.full(chain_count, -1, np.int32))
            groups.append(group)
        group["sources"].append(source)
        group["targets"].append(target)
        group["start"][source] = plane_count - count if way == 1 else 0
        group["arrives"][target] = plane_count + own_slot[target] + (-count if way == 1 else plane_count)
    return band_planes, own_slot, bounds, sides, groups


def two_sided(field):
    return (
        pltpu.roll(field, 1, 0) + pltpu.roll(field, field.shape[0] - 1, 0)
        + pltpu.roll(field, 1, 1) + pltpu.roll(field, field.shape[1] - 1, 1)
    )


def laplace_kernel(counts, planes, lines, band, vectors, table, *refs):
    groups = len(counts)
    own, own_marks, edge, edge_marks = refs[:4]
    got = refs[4 : 4 + 4 * groups]
    image, gram, field, mark, scale, degree, once, kept = refs[4 + 4 * groups :]
    k = pl.program_id(0)
    window = band + 2 * REACH

    def place(dest, start, count, body, border):
        dest[pl.ds(start, count), 0:lines, :] = body
        dest[pl.ds(start, count), lines : lines + REACH, :] = border[:, 0:REACH]
        dest[pl.ds(start, count), lines + 8 - REACH : lines + 8, :] = border[:, REACH:]

    def gather(dest, body, border, which):
        place(dest, planes + table[0], planes, body, border)
        for g in range(groups):
            start = table[4 + g]

            @pl.when(start >= 0)
            def _():
                place(dest, start, counts[g], got[4 * g + which][0], got[4 * g + 2 + which][0])

    @pl.when(k == 0)
    def _():
        mark[...] = jnp.full(mark.shape, -1.0, jnp.float32)
        gather(mark, own_marks[...].astype(jnp.float32), edge_marks[0], 1)
        side = table[3].astype(jnp.float32)
        for s in range(window):
            inside = (s >= table[1]) & (s < table[2])
            here = jnp.where(inside, side, jnp.float32(-2.0))
            mark[planes + s] = (mark[planes + s] == here).astype(jnp.float32)
        for s in range(1, window - 1):
            at = planes + s
            total = mark[at - 1] + mark[at + 1] + two_sided(mark[at])
            scale[s] = mark[at] / 6.0
            degree[s] = mark[at] * total / 6.0

    gather(field, own[0], edge[0], 0)

    def moved(s):
        return jnp.where(mark[planes + s] > 0.5, field[planes + s], 0.0)

    before, here = moved(0), moved(1)
    for s in range(1, window - 1):
        after = moved(s + 1)
        value = degree[s] * here - scale[s] * (before + after + two_sided(here))
        once[s] = value
        if REACH <= s < window - REACH:
            kept[pl.ds((s - REACH) * lines * vectors + k, lines, stride=vectors), :] = value[0:lines]
        before, here = here, after
    for s in range(REACH, window - REACH):
        value = once[s]
        result = degree[s] * value - scale[s] * (once[s - 1] + once[s + 1] + two_sided(value))
        image[0, s - REACH] = result[0:lines]

    @pl.when(k == vectors - 1)
    def _():
        rows = 8 * vectors
        steps = band * lines // 8

        def add(step, total):
            block = kept[pl.ds(pl.multiple_of(step * rows, rows), rows), :]
            high = block.astype(jnp.bfloat16)
            low = (block - high.astype(jnp.float32)).astype(jnp.bfloat16)
            dot = functools.partial(
                lax.dot_general, dimension_numbers=(((1,), (1,)), ((), ())), preferred_element_type=jnp.float32
            )
            return total + dot(high, high) + (dot(high, low) + dot(low, high))

        total = lax.fori_loop(0, steps, add, jnp.zeros((rows, rows), jnp.float32), unroll=2)
        gram[...] = total


def per_device(fiedler, side_labels):
    chain_count, lane_count = lax.axis_size("chain"), lax.axis_size("lane")
    vectors, plane_count, lines, width = fiedler.shape
    band, own_slot, bounds, sides, groups = band_plan(chain_count, plane_count)
    me = lax.axis_index("chain")
    marks = side_labels.astype(jnp.float32)[None]

    def both(part):
        return jnp.concatenate([part(fiedler), part(marks)], axis=0)

    up = [(i, (i + 1) % lane_count) for i in range(lane_count)]
    down = [(j, i) for i, j in up]
    after = lax.ppermute(both(lambda a: a[:, :, :REACH]), "lane", down)
    before = lax.ppermute(both(lambda a: a[:, :, lines - REACH :]), "lane", up)
    edge = jnp.concatenate([after, before], axis=2)

    counts = tuple(group["count"] for group in groups)
    got, edges_got = [], []
    for group in groups:
        start = jnp.asarray(group["start"])[me]
        pairs = list(zip(group["sources"], group["targets"]))
        count = group["count"]
        cut = functools.partial(lax.dynamic_slice_in_dim, start_index=start, slice_size=count, axis=1)
        got.append(lax.ppermute(both(cut), "chain", pairs))
        edges_got.append(lax.ppermute(cut(edge), "chain", pairs))

    rows = np.stack([own_slot, bounds[0], bounds[1], sides] + [group["arrives"] for group in groups])
    table = jnp.asarray(rows)[:, me]

    def spec(shape, at):
        return pl.BlockSpec((1,) + shape[1:], lambda k, t: (k if at is None else at, 0, 0, 0))

    operands = [fiedler, side_labels, edge, edge]
    in_specs = [
        spec(fiedler.shape, None),
        pl.BlockSpec(side_labels.shape, lambda k, t: (0, 0, 0)),
        spec(edge.shape, None),
        spec(edge.shape, vectors),
    ]
    for body, border in zip(got, edges_got):
        operands += [body, body, border, border]
        in_specs += [spec(body.shape, None), spec(body.shape, vectors)]
        in_specs += [spec(border.shape, None), spec(border.shape, vectors)]
    window = band + 2 * REACH
    tall = lines + 8
    held = (plane_count * 2 + window, tall, width)
    image, wide = pl.pallas_call(
        functools.partial(laplace_kernel, counts, plane_count, lines, band, vectors),
        grid_spec=pltpu.PrefetchScalarGridSpec(
            num_scalar_prefetch=1,
            grid=(vectors,),
            in_specs=in_specs,
            out_specs=[
                pl.BlockSpec((1, band, lines, width), lambda k, t: (k, 0, 0, 0)),
                pl.BlockSpec((8 * vectors, 8 * vectors), lambda k, t: (0, 0)),
            ],
            scratch_shapes=[
                pltpu.VMEM(held, jnp.float32),
                pltpu.VMEM(held, jnp.float32),
                pltpu.VMEM((window, tall, width), jnp.float32),
                pltpu.VMEM((window, tall, width), jnp.float32),
                pltpu.VMEM((window, tall, width), jnp.float32),
                pltpu.VMEM((band * lines * vectors, width), jnp.float32),
            ],
        ),
        out_shape=[
            jax.ShapeDtypeStruct((vectors, band, lines, width), jnp.float32),
            jax.ShapeDtypeStruct((8 * vectors, 8 * vectors), jnp.float32),
        ],
        compiler_params=pltpu.CompilerParams(
            dimension_semantics=("arbitrary",), vmem_limit_bytes=48 * 1024 * 1024
        ),
        name="laplace",
    )(table, *operands)
    local = jnp.einsum("akal->kl", wide.reshape(8, vectors, 8, vectors))
    slots = band * (chain_count // 2) * lines * lane_count * width
    mine = jnp.arange(2, dtype=jnp.int32)[:, None, None] == jnp.asarray(sides)[me]
    blocks = jnp.where(mine, local[None] / slots, jnp.float32(0.0))
    return image, lax.psum(blocks, ("chain", "lane"))


def solution(mesh):
    return jax.shard_map(
        per_device,
        mesh=mesh,
        in_specs=(P(None, "chain", "lane", None), P("chain", "lane", None)),
        out_specs=(P(None, "chain", "lane", None), P()),
        check_vma=False,
    )
```

profile of v0, /device:TPU:0, one launch (start us, length us, event | category | flops | bytes accessed | tf_op | source)
XLA Modules:
  0.0 112.4 jit_solution(5284722731400982012)
XLA Ops:
  0.6 1.2 %dynamic_slice.43 = s32[1]{0:T(128)} dynamic-slice(s32[8]{0:T(128)} %constant.28.clone, s32[]{:T(128)S(6)} %select_n.13), dynamic_slice_sizes={1} | dynamic-slice | bytes 12 | tf_op jit(solution)/shard_map/dynamic_slice | solution.py:154
  3.2 1.0 fusion.5
  4.8 1.6 %constant_dynamic-slice_fusion.2 = f32[16,6,32,128]{3,2,1,0:T(8,128)S(1)} fusion(f32[16,12,32,128]{3,2,1,0:T(8,128)} %refs_0_.1, s32[]{:T(128)S(6)} %select_n.14), kind=kLoop, calls=%fused_computation.24 | loop fusion | bytes 3145732 | tf_op jit(solution)/shard_map/dynamic_slice | solution.py:143
  6.4 1.4 %pad_maximum_fusion = f32[17,6,32,128]{3,2,1,0:T(8,128)} fusion(f32[1,6,32,128]{3,2,1,0:T(8,128)S(1)} %dynamic-slice_bitcast_fusion, f32[16,6,32,128]{3,2,1,0:T(8,128)S(1)} %constant_dynamic-slice_fusion.2), kind=kLoop, calls=%fused_computation | loop fusion | flops 417792 | bytes 3342336 | tf_op jit(solution)/shard_map/concatenate | solution.py:143
  7.8 0.8 collective-permute-start.2
  8.6 0.6 dynamic_slice.47
  11.1 1.4 %constant_dynamic-slice_fusion.1 = f32[16,5,32,128]{3,2,1,0:T(8,128)S(1)} fusion(f32[16,12,32,128]{3,2,1,0:T(8,128)} %refs_0_.1, s32[]{:T(128)S(6)} %select_n.15), kind=kLoop, calls=%fused_computation.23 | loop fusion | bytes 2621444 | tf_op jit(solution)/shard_map/dynamic_slice | solution.py:143
  12.6 1.2 %pad_maximum_fusion.1 = f32[17,5,32,128]{3,2,1,0:T(8,128)} fusion(f32[1,5,32,128]{3,2,1,0:T(8,128)S(1)} %dynamic-slice_bitcast_fusion.1, f32[16,5,32,128]{3,2,1,0:T(8,128)S(1)} %constant_dynamic-slice_fusion.1), kind=kLoop, calls=%fused_computation.1 | loop fusion | flops 348160 | bytes 2785280 | tf_op jit(solution)/shard_map/concatenate | solution.py:143
  13.8 1.3 %collective-permute-start.4 = (f32[17,5,32,128]{3,2,1,0:T(8,128)}, f32[17,5,32,128]{3,2,1,0:T(8,128)S(1)}, u32[]{:S(2)}, u32[]{:S(2)}) collective-permute-start(f32[17,5,32,128]{3,2,1,0:T(8,128)} %pad_maximum_fusion.1), channel_id=1, source_target_pairs={{24,28},{20,16},{8,12},{4,0},{25,29},{21,17},{9,13},{5,1},{26,30},... | collective-permute-start | bytes 4177928 | tf_op jit(solution)/shard_map/ppermute | solution.py:158
  15.1 0.6 dynamic_slice.51
  17.6 1.1 constant_dynamic-slice_fusion
  18.8 5.3 %collective-permute-start.6 = (f32[17,2,32,128]{3,2,1,0:T(8,128)S(1)}, f32[17,2,32,128]{3,2,1,0:T(8,128)S(1)}, u32[]{:S(2)}, u32[]{:S(2)}) collective-permute-start(f32[17,2,32,128]{3,2,1,0:T(8,128)S(1)} %pad_maximum_fusion.3), channel_id=1, source_target_pairs={{28,0},{16,12},{12,16},{0,28},{29,1},{17,13},{13,17},{1,29},{30,2}... | collective-permute-start | bytes 1671176 | tf_op jit(solution)/shard_map/ppermute | solution.py:158
  24.1 1.5 %fusion.4 = (f32[16,12,2,128]{3,2,1,0:T(2,128)S(1)}, f32[16,12,2,128]{3,2,1,0:T(2,128)S(1)}) fusion(f32[16,12,32,128]{3,2,1,0:T(8,128)} %refs_0_.1), kind=kLoop, calls=%fused_computation.29 | loop fusion | bytes 786432 | tf_op jit(solution)/shard_map/slice | solution.py:147
  25.6 0.1 pad_maximum_fusion.4
  25.7 3.7 %collective-permute-start = (f32[17,12,2,128]{3,2,1,0:T(2,128)S(1)}, f32[17,12,2,128]{3,2,1,0:T(2,128)S(1)}, u32[]{:S(2)}, u32[]{:S(2)}) collective-permute-start(f32[17,12,2,128]{3,2,1,0:T(2,128)S(1)} %pad_maximum_fusion.4), channel_id=1, source_target_pairs={{1,0},{2,1},{3,2},{0,3},{5,4},{6,5},{7,6},{4,7},{9,8},{10,9},{11,1... | collective-permute-start | bytes 626696 | tf_op jit(solution)/shard_map/ppermute | solution.py:147
  29.4 0.1 pad_maximum_fusion.5
  29.5 0.6 dynamic_slice.55
  30.1 0.7 fusion.3.table
  30.8 4.1 %collective-permute-done = f32[17,12,2,128]{3,2,1,0:T(2,128)S(1)} collective-permute-done((f32[17,12,2,128]{3,2,1,0:T(2,128)S(1)}, f32[17,12,2,128]{3,2,1,0:T(2,128)S(1)}, u32[]{:S(2)}, u32[]{:S(2)}) %collective-permute-start) | collective-permute-done | bytes 208928 | tf_op jit(solution)/shard_map/ppermute | solution.py:147
  34.9 4.2 %collective-permute-done.1 = f32[17,12,2,128]{3,2,1,0:T(2,128)S(1)} collective-permute-done((f32[17,12,2,128]{3,2,1,0:T(2,128)S(1)}, f32[17,12,2,128]{3,2,1,0:T(2,128)S(1)}, u32[]{:S(2)}, u32[]{:S(2)}) %collective-permute-start.1) | collective-permute-done | bytes 208928 | tf_op jit(solution)/shard_map/ppermute | solution.py:148
  39.1 0.1 fusion
  39.2 0.7 collective-permute-start.3
  39.9 2.6 %collective-permute-start.7 = (f32[17,2,4,128]{3,2,1,0:T(4,128)S(1)}, f32[17,2,4,128]{3,2,1,0:T(4,128)S(1)}, u32[]{:S(2)}, u32[]{:S(2)}) collective-permute-start(f32[17,2,4,128]{3,2,1,0:T(4,128)S(1)} %fusion.2), channel_id=1, source_target_pairs={{28,0},{16,12},{12,16},{0,28},{29,1},{17,13},{13,17},{1,29},{30,2}... | collective-permute-start | bytes 208904 | tf_op jit(solution)/shard_map/ppermute | solution.py:159
  42.6 4.5 %collective-permute-done.7.refs_14_.refs_15_ = f32[17,2,4,128]{3,2,1,0:T(4,128)S(1)} collective-permute-done((f32[17,2,4,128]{3,2,1,0:T(4,128)S(1)}, f32[17,2,4,128]{3,2,1,0:T(4,128)S(1)}, u32[]{:S(2)}, u32[]{:S(2)}) %collective-permute-start.7) | collective-permute-done | bytes 69664 | tf_op jit(solution)/shard_map/ppermute | solution.py:159
  47.2 1.3 %collective-permute-start.5 = (f32[17,5,4,128]{3,2,1,0:T(4,128)S(1)}, f32[17,5,4,128]{3,2,1,0:T(4,128)S(1)}, u32[]{:S(2)}, u32[]{:S(2)}) collective-permute-start(f32[17,5,4,128]{3,2,1,0:T(4,128)S(1)} %fusion.1), channel_id=1, source_target_pairs={{24,28},{20,16},{8,12},{4,0},{25,29},{21,17},{9,13},{5,1},{26,30},... | collective-permute-start | bytes 522248 | tf_op jit(solution)/shard_map/ppermute | solution.py:159
  48.5 0.7 iota_compare_fusion.1
  49.1 0.2 pad_maximum_fusion.2.refs_2_.refs_3_
  49.3 1.1 %collective-permute-done.5.refs_10_.refs_11_ = f32[17,5,4,128]{3,2,1,0:T(4,128)S(1)} collective-permute-done((f32[17,5,4,128]{3,2,1,0:T(4,128)S(1)}, f32[17,5,4,128]{3,2,1,0:T(4,128)S(1)}, u32[]{:S(2)}, u32[]{:S(2)}) %collective-permute-start.5) | collective-permute-done | bytes 174112 | tf_op jit(solution)/shard_map/ppermute | solution.py:159
  50.5 22.1 %laplace.1 = (f32[16,15,32,128]{3,2,1,0:T(8,128)}, f32[128,128]{1,0:T(8,128)S(1)}) custom-call(s32[7]{0:T(128)S(1)} %fusion.3.table, f32[16,12,32,128]{3,2,1,0:T(8,128)} %refs_0_.1, s32[12,32,128]{2,1,0:T(8,128)S(1)} %copy-done, f32[17,12,4,128]{3,2,1,0:T(4,128)S(1)} %pad_maximum_fusion.2.refs_2_.refs_3_, ...), custom_call_target="tpu_custom_call" | custom-call | tf_op jit(solution)/shard_map/laplace/pallas_call | solution.py:181
  72.6 0.2 reshape.19
  72.8 0.1 select_reduce_fusion
  73.0 39.4 %psum.7 = f32[2,16,16]{2,1,0:T(8,128)} all-reduce(f32[2,16,16]{2,1,0:T(8,128)S(1)} %broadcast_select_fusion), channel_id=1, replica_groups=mesh['chain'=8,'lane'=4] {'chain','lane'}, use_global_device_ids=true, to_apply=%region_1.2 | all-reduce | flops 512 | bytes 4096 | tf_op jit(solution)/shard_map/psum | solution.py:213
  (23 shorter events, 0.4 us)
Async XLA Ops:
  6.4 2.1 %copy-start.3 = (s32[8]{0:T(128)S(1)}, s32[8]{0:T(128)}, u32[]{:S(2)}) copy-start(s32[8]{0:T(128)} %constant.29.clone) | copy-start | bytes 100
  7.8 42.7 %collective-permute-start.2 = (f32[17,6,32,128]{3,2,1,0:T(8,128)}, f32[17,6,32,128]{3,2,1,0:T(8,128)S(1)}, u32[]{:S(2)}, u32[]{:S(2)}) collective-permute-start(f32[17,6,32,128]{3,2,1,0:T(8,128)} %pad_maximum_fusion), channel_id=1, source_target_pairs={{24,20},{20,24},{8,4},{4,8},{25,21},{21,25},{9,5},{5,9},{26,22},{2... | collective-permute-start | bytes 5013512 | tf_op jit(solution)/shard_map/ppermute | solution.py:158
  12.5 2.5 %copy-start.2 = (s32[8]{0:T(128)S(1)}, s32[8]{0:T(128)}, u32[]{:S(2)}) copy-start(s32[8]{0:T(128)} %constant.30.clone) | copy-start | bytes 100
  13.8 36.7 %collective-permute-start.4 = (f32[17,5,32,128]{3,2,1,0:T(8,128)}, f32[17,5,32,128]{3,2,1,0:T(8,128)S(1)}, u32[]{:S(2)}, u32[]{:S(2)}) collective-permute-start(f32[17,5,32,128]{3,2,1,0:T(8,128)} %pad_maximum_fusion.1), channel_id=1, source_target_pairs={{24,28},{20,16},{8,12},{4,0},{25,29},{21,17},{9,13},{5,1},{26,30},... | collective-permute-start | bytes 4177928 | tf_op jit(solution)/shard_map/ppermute | solution.py:158
  18.7 10.8 %copy-start.1 = (s32[8]{0:T(128)S(1)}, s32[8]{0:T(128)}, u32[]{:S(2)}) copy-start(s32[8]{0:T(128)} %constant.32.clone) | copy-start | bytes 100
  18.8 31.7 %collective-permute-start.6 = (f32[17,2,32,128]{3,2,1,0:T(8,128)S(1)}, f32[17,2,32,128]{3,2,1,0:T(8,128)S(1)}, u32[]{:S(2)}, u32[]{:S(2)}) collective-permute-start(f32[17,2,32,128]{3,2,1,0:T(8,128)S(1)} %pad_maximum_fusion.3), channel_id=1, source_target_pairs={{28,0},{16,12},{12,16},{0,28},{29,1},{17,13},{13,17},{1,29},{30,2}... | collective-permute-start | bytes 1671176 | tf_op jit(solution)/shard_map/ppermute | solution.py:158
  25.6 24.9 %copy-start = (s32[12,32,128]{2,1,0:T(8,128)S(1)}, s32[12,32,128]{2,1,0:T(8,128)}, u32[]{:S(2)}) copy-start(s32[12,32,128]{2,1,0:T(8,128)} %refs_1_.1) | copy-start | bytes 589828
  25.7 9.2 %collective-permute-start = (f32[17,12,2,128]{3,2,1,0:T(2,128)S(1)}, f32[17,12,2,128]{3,2,1,0:T(2,128)S(1)}, u32[]{:S(2)}, u32[]{:S(2)}) collective-permute-start(f32[17,12,2,128]{3,2,1,0:T(2,128)S(1)} %pad_maximum_fusion.4), channel_id=1, source_target_pairs={{1,0},{2,1},{3,2},{0,3},{5,4},{6,5},{7,6},{4,7},{9,8},{10,9},{11,1... | collective-permute-start | bytes 626696 | tf_op jit(solution)/shard_map/ppermute | solution.py:147
  29.5 9.6 %collective-permute-start.1 = (f32[17,12,2,128]{3,2,1,0:T(2,128)S(1)}, f32[17,12,2,128]{3,2,1,0:T(2,128)S(1)}, u32[]{:S(2)}, u32[]{:S(2)}) collective-permute-start(f32[17,12,2,128]{3,2,1,0:T(2,128)S(1)} %pad_maximum_fusion.5), channel_id=1, source_target_pairs={{0,1},{1,2},{2,3},{3,0},{4,5},{5,6},{6,7},{7,4},{8,9},{9,10},{10,1... | collective-permute-start | bytes 626696 | tf_op jit(solution)/shard_map/ppermute | solution.py:148
  39.2 11.3 %collective-permute-start.3 = (f32[17,6,4,128]{3,2,1,0:T(4,128)S(1)}, f32[17,6,4,128]{3,2,1,0:T(4,128)S(1)}, u32[]{:S(2)}, u32[]{:S(2)}) collective-permute-start(f32[17,6,4,128]{3,2,1,0:T(4,128)S(1)} %fusion), channel_id=1, source_target_pairs={{24,20},{20,24},{8,4},{4,8},{25,21},{21,25},{9,5},{5,9},{26,22},{2... | collective-permute-start | bytes 626696 | tf_op jit(solution)/shard_map/ppermute | solution.py:159
  39.9 7.3 %collective-permute-start.7 = (f32[17,2,4,128]{3,2,1,0:T(4,128)S(1)}, f32[17,2,4,128]{3,2,1,0:T(4,128)S(1)}, u32[]{:S(2)}, u32[]{:S(2)}) collective-permute-start(f32[17,2,4,128]{3,2,1,0:T(4,128)S(1)} %fusion.2), channel_id=1, source_target_pairs={{28,0},{16,12},{12,16},{0,28},{29,1},{17,13},{13,17},{1,29},{30,2}... | collective-permute-start | bytes 208904 | tf_op jit(solution)/shard_map/ppermute | solution.py:159
  47.2 3.3 %collective-permute-start.5 = (f32[17,5,4,128]{3,2,1,0:T(4,128)S(1)}, f32[17,5,4,128]{3,2,1,0:T(4,128)S(1)}, u32[]{:S(2)}, u32[]{:S(2)}) collective-permute-start(f32[17,5,4,128]{3,2,1,0:T(4,128)S(1)} %fusion.1), channel_id=1, source_target_pairs={{24,28},{20,16},{8,12},{4,0},{25,29},{21,17},{9,13},{5,1},{26,30},... | collective-permute-start | bytes 522248 | tf_op jit(solution)/shard_map/ppermute | solution.py:159
where the time goes:
time: 113 us; the launch traced here: 112 us
  blocking collectives  39.4 us (35%)
  Pallas kernels  22.1 us (20%)
  starting transfers between devices  15.6 us (14%)
  waiting for transfers between devices  13.9 us (12%)
  local copies, waits for them, and re-layouts  9.57 us (8%)
  between operations  6.75 us (6%)
  other arithmetic  5.06 us (4%)
    psum x1, blocking collectives, per_device(): return (image, lax.psum(blocks, ('chain', 'lane')))  39.4 us
    pallas_call x1, Pallas kernels, per_device(): pl.pallas_call(functools.partial(laplace_kernel, counts, plane_count, lin...  22.1 us
    ppermute x3, starting transfers between devices, per_device(): got.append(lax.ppermute(both(cut), 'chain', pairs))  7.31 us
    ppermute x3, waiting for transfers between devices, per_device(): edges_got.append(lax.ppermute(cut(edge), 'chain', pairs))  5.67 us
    ppermute x3, starting transfers between devices, per_device(): edges_got.append(lax.ppermute(cut(edge), 'chain', pairs))  4.6 us
    ppermute x1, waiting for transfers between devices, per_device(): before = lax.ppermute(both(lambda a: a[:, :, lines - REACH:]), 'lane', up)  4.15 us
    dynamic_slice x6, local copies, waits for them, and re-layouts, both(): return jnp.concatenate([part(fiedler), part(marks)], axis=0)  4.12 us
    ppermute x1, waiting for transfers between devices, per_device(): after = lax.ppermute(both(lambda a: a[:, :, :REACH]), 'lane', down)  4.09 us
  transfers between devices with their start and end apart: 8, of which 4 were waited for; matrix products, arithmetic and copies ran while one was open for 8% of the time, Pallas kernels for 0%

commit v1 on v0

--- a/solution.py
+++ b/solution.py
@@ -59,7 +59,7 @@
     )
 
 
-def laplace_kernel(counts, planes, lines, band, vectors, table, *refs):
+def laplace_kernel(counts, planes, lines, band, vectors, slots, table, *refs):
     groups = len(counts)
     own, own_marks, edge, edge_marks = refs[:4]
     got = refs[4 : 4 + 4 * groups]
@@ -129,7 +129,58 @@
             return total + dot(high, high) + (dot(high, low) + dot(low, high))
 
         total = lax.fori_loop(0, steps, add, jnp.zeros((rows, rows), jnp.float32), unroll=2)
-        gram[...] = total
+        row = lax.broadcasted_iota(jnp.int32, total.shape, 0) // vectors
+        column = lax.broadcasted_iota(jnp.int32, total.shape, 1) // vectors
+        total = jnp.where(row == column, total, 0.0)
+        folded = total[0:vectors]
+        for part in range(1, 8):
+            folded = folded + total[part * vectors : (part + 1) * vectors]
+        shift = rows // 2
+        while shift >= vectors:
+            folded = folded + pltpu.roll(folded, shift, 1)
+            shift //= 2
+        gram[...] = folded / slots
+
+
+def gram_sum_kernel(sides, lane_count, local, out, lane_got, total, chain_got, *sems):
+    chain_count = len(sides)
+    my_chain, my_lane = lax.axis_index("chain"), lax.axis_index("lane")
+    barrier = pltpu.get_barrier_semaphore()
+    for d in range(1, lane_count):
+        pl.semaphore_signal(barrier, inc=1, device_id=(my_chain, (my_lane + d) % lane_count),
+                            device_id_type=pl.DeviceIdType.MESH)
+    for d in range(1, chain_count):
+        pl.semaphore_signal(barrier, inc=1, device_id=((my_chain + d) % chain_count, my_lane),
+                            device_id_type=pl.DeviceIdType.MESH)
+    pl.semaphore_wait(barrier, lane_count + chain_count - 2)
+
+    def gather(src, got, me, count, device, send, recv):
+        def copy(d, slot):
+            return pltpu.make_async_remote_copy(
+                src_ref=src, dst_ref=got.at[slot], send_sem=send.at[d], recv_sem=recv.at[d],
+                device_id=device((me + d) % count), device_id_type=pl.DeviceIdType.MESH,
+            )
+
+        for d in range(1, count):
+            copy(d, me).start()
+        got[me] = src[...]
+        for d in range(1, count):
+            copy(d, (me + count - d) % count).wait_recv()
+        for d in range(1, count):
+            copy(d, me).wait_send()
+
+    gather(local, lane_got, my_lane, lane_count, lambda i: (my_chain, i), sems[0], sems[1])
+    value = lane_got[0]
+    for i in range(1, lane_count):
+        value = value + lane_got[i]
+    total[...] = value
+    gather(total, chain_got, my_chain, chain_count, lambda i: (i, my_lane), sems[2], sems[3])
+    for side in range(2):
+        members = [c for c in range(chain_count) if sides[c] == side]
+        value = chain_got[members[0]]
+        for c in members[1:]:
+            value = value + chain_got[c]
+        out[side] = value
 
 
 def per_device(fiedler, side_labels):
@@ -137,6 +188,13 @@
     vectors, plane_count, lines, width = fiedler.shape
     band, own_slot, bounds, sides, groups = band_plan(chain_count, plane_count)
     me = lax.axis_index("chain")
+    slots = band * (chain_count // 2) * lines * lane_count * width
+    rows = np.stack(
+        [own_slot, bounds[0], bounds[1], sides]
+        + [group["arrives"] for group in groups]
+        + [group["start"] for group in groups]
+    )
+    table = lax.optimization_barrier(jnp.asarray(rows.T)[me])
     marks = side_labels.astype(jnp.float32)[None]
 
     def both(part):
@@ -150,16 +208,13 @@
 
     counts = tuple(group["count"] for group in groups)
     got, edges_got = [], []
-    for group in groups:
-        start = jnp.asarray(group["start"])[me]
+    for which, group in enumerate(groups):
+        start = table[4 + len(groups) + which]
         pairs = list(zip(group["sources"], group["targets"]))
         count = group["count"]
         cut = functools.partial(lax.dynamic_slice_in_dim, start_index=start, slice_size=count, axis=1)
         got.append(lax.ppermute(both(cut), "chain", pairs))
         edges_got.append(lax.ppermute(cut(edge), "chain", pairs))
-
-    rows = np.stack([own_slot, bounds[0], bounds[1], sides] + [group["arrives"] for group in groups])
-    table = jnp.asarray(rows)[:, me]
 
     def spec(shape, at):
         return pl.BlockSpec((1,) + shape[1:], lambda k, t: (k if at is None else at, 0, 0, 0))
@@ -179,14 +234,14 @@
     tall = lines + 8
     held = (plane_count * 2 + window, tall, width)
     image, wide = pl.pallas_call(
-        functools.partial(laplace_kernel, counts, plane_count, lines, band, vectors),
+        functools.partial(laplace_kernel, counts, plane_count, lines, band, vectors, float(slots)),
         grid_spec=pltpu.PrefetchScalarGridSpec(
             num_scalar_prefetch=1,
             grid=(vectors,),
             in_specs=in_specs,
             out_specs=[
                 pl.BlockSpec((1, band, lines, width), lambda k, t: (k, 0, 0, 0)),
-                pl.BlockSpec((8 * vectors, 8 * vectors), lambda k, t: (0, 0)),
+                pl.BlockSpec((vectors, 8 * vectors), lambda k, t: (0, 0)),
             ],
             scratch_shapes=[
                 pltpu.VMEM(held, jnp.float32),
@@ -199,18 +254,32 @@
         ),
         out_shape=[
             jax.ShapeDtypeStruct((vectors, band, lines, width), jnp.float32),
-            jax.ShapeDtypeStruct((8 * vectors, 8 * vectors), jnp.float32),
+            jax.ShapeDtypeStruct((vectors, 8 * vectors), jnp.float32),
         ],
         compiler_params=pltpu.CompilerParams(
             dimension_semantics=("arbitrary",), vmem_limit_bytes=48 * 1024 * 1024
         ),
         name="laplace",
     )(table, *operands)
-    local = jnp.einsum("akal->kl", wide.reshape(8, vectors, 8, vectors))
-    slots = band * (chain_count // 2) * lines * lane_count * width
-    mine = jnp.arange(2, dtype=jnp.int32)[:, None, None] == jnp.asarray(sides)[me]
-    blocks = jnp.where(mine, local[None] / slots, jnp.float32(0.0))
-    return image, lax.psum(blocks, ("chain", "lane"))
+    shape = wide.shape
+    sums = pl.pallas_call(
+        functools.partial(gram_sum_kernel, tuple(int(side) for side in sides), lane_count),
+        out_shape=jax.ShapeDtypeStruct((2,) + shape, jnp.float32),
+        in_specs=[pl.BlockSpec(memory_space=pltpu.VMEM)],
+        out_specs=pl.BlockSpec(memory_space=pltpu.VMEM),
+        scratch_shapes=[
+            pltpu.VMEM((lane_count,) + shape, jnp.float32),
+            pltpu.VMEM(shape, jnp.float32),
+            pltpu.VMEM((chain_count,) + shape, jnp.float32),
+            pltpu.SemaphoreType.DMA((lane_count,)),
+            pltpu.SemaphoreType.DMA((lane_count,)),
+            pltpu.SemaphoreType.DMA((chain_count,)),
+            pltpu.SemaphoreType.DMA((chain_count,)),
+        ],
+        compiler_params=pltpu.CompilerParams(collective_id=0, has_side_effects=True),
+        name="gram_sum",
+    )(wide)
+    return image, sums[:, :, :vectors]
 
 
 def solution(mesh):

time: 113 us -> 82 us (0.73)
  blocking collectives: 39.4 us -> 0 us
  Pallas kernels: 22.1 us -> 35.4 us
  waiting for transfers between devices: 13.9 us -> 8.09 us
    psum x1 -> x0, blocking collectives: 39.4 us -> none  [per_device(): return (image, lax.psum(blocks, ('chain', 'lane')))]
    pallas_call x0 -> x1, Pallas kernels: none -> 13.1 us  [per_device(): pl.pallas_call(functools.partial(gram_sum_kernel, tuple((int(side) for si...]
    ppermute x1, waiting for transfers between devices: 4.15 us -> 0.01 us  [per_device(): before = lax.ppermute(both(lambda a: a[:, :, lines - REACH:]), 'lane', up)]
    dynamic_slice x4 -> x0, local copies, waits for them, and re-layouts: 3.01 us -> none  [the longest x3 2.42 us: per_device(): start = jnp.asarray(group['start'])[me]]
    ppermute x1, starting transfers between devices: 0.06 us -> 3.05 us  [per_device(): before = lax.ppermute(both(lambda a: a[:, :, lines - REACH:]), 'lane', up)]
    unnamed x8 -> x7, local copies, waits for them, and re-layouts: 0.03 us -> 1.93 us
    ppermute x1, waiting for transfers between devices: 4.09 us -> 2.28 us  [per_device(): after = lax.ppermute(both(lambda a: a[:, :, :REACH]), 'lane', down)]
    ppermute x1, starting transfers between devices: 3.65 us -> 2.03 us  [per_device(): after = lax.ppermute(both(lambda a: a[:, :, :REACH]), 'lane', down)]
  transfers between devices with their start and end apart: 8 -> 8, of which waited for: 4 -> 3; matrix products, arithmetic and copies ran while one was open for 8% -> 10% of each run, Pallas kernels for 0% -> 0%
where the time goes in v1:
time: 82 us; the launch traced here: 81 us
  Pallas kernels  35.4 us (43%)
  starting transfers between devices  15.7 us (19%)
  local copies, waits for them, and re-layouts  9.7 us (12%)
  waiting for transfers between devices  8.09 us (10%)
  between operations  6.58 us (8%)
  other arithmetic  5.58 us (7%)
    pallas_call x1, Pallas kernels, per_device(): pl.pallas_call(functools.partial(laplace_kernel, counts, plane_count, lin...  22.3 us
    pallas_call x1, Pallas kernels, per_device(): pl.pallas_call(functools.partial(gram_sum_kernel, tuple((int(side) for si...  13.1 us
    ppermute x3, waiting for transfers between devices, per_device(): edges_got.append(lax.ppermute(cut(edge), 'chain', pairs))  5.8 us
    ppermute x3, starting transfers between devices, per_device(): got.append(lax.ppermute(both(cut), 'chain', pairs))  5.68 us
    ppermute x3, starting transfers between devices, per_device(): edges_got.append(lax.ppermute(cut(edge), 'chain', pairs))  4.91 us
    dynamic_slice x6, local copies, waits for them, and re-layouts, both(): return jnp.concatenate([part(fiedler), part(marks)], axis=0)  4.88 us
    concatenate x5, other arithmetic, both(): return jnp.concatenate([part(fiedler), part(marks)], axis=0)  4.19 us
    ppermute x1, starting transfers between devices, per_device(): before = lax.ppermute(both(lambda a: a[:, :, lines - REACH:]), 'lane', up)  3.05 us
  transfers between devices with their start and end apart: 8, of which 3 were waited for; matrix products, arithmetic and copies ran while one was open for 10% of the time, Pallas kernels for 0%

profile of v1, /device:TPU:0, one launch (start us, length us, event | category | flops | bytes accessed | tf_op | source)
XLA Modules:
  0.0 81.0 jit_solution(14687850125260202353)
XLA Ops:
  0.6 0.7 fusion.3.table
  1.3 0.6 fusion.7
  3.3 1.0 %fusion.5 = (f32[12,32,128]{2,1,0:T(8,128)S(1)}, f32[1,12,32,128]{3,2,1,0:T(8,128)S(1)}) fusion(s32[12,32,128]{2,1,0:T(8,128)} %refs_1_.1), kind=kLoop, calls=%fused_computation.25 | loop fusion | flops 49152 | bytes 589824 | tf_op jit(solution)/shard_map/convert_element_type | solution.py:198
  4.9 1.6 %constant_dynamic-slice_fusion.2 = f32[16,6,32,128]{3,2,1,0:T(8,128)S(1)} fusion(f32[16,12,32,128]{3,2,1,0:T(8,128)} %refs_0_.1, s32[]{:T(128)S(6)} %select_n.9), kind=kLoop, calls=%fused_computation.20 | loop fusion | bytes 3145732 | tf_op jit(solution)/shard_map/dynamic_slice | solution.py:201
  6.5 1.4 %pad_maximum_fusion = f32[17,6,32,128]{3,2,1,0:T(8,128)} fusion(f32[1,6,32,128]{3,2,1,0:T(8,128)S(1)} %dynamic-slice_bitcast_fusion, f32[16,6,32,128]{3,2,1,0:T(8,128)S(1)} %constant_dynamic-slice_fusion.2), kind=kLoop, calls=%fused_computation | loop fusion | flops 417792 | bytes 3342336 | tf_op jit(solution)/shard_map/concatenate | solution.py:201
  7.9 0.8 collective-permute-start.2
  10.5 1.4 %constant_dynamic-slice_fusion.1 = f32[16,5,32,128]{3,2,1,0:T(8,128)S(1)} fusion(f32[16,12,32,128]{3,2,1,0:T(8,128)} %refs_0_.1, s32[]{:T(128)S(6)} %select_n.20), kind=kLoop, calls=%fused_computation.19 | loop fusion | bytes 2621444 | tf_op jit(solution)/shard_map/dynamic_slice | solution.py:201
  12.0 1.2 %pad_maximum_fusion.1 = f32[17,5,32,128]{3,2,1,0:T(8,128)} fusion(f32[1,5,32,128]{3,2,1,0:T(8,128)S(1)} %dynamic-slice_bitcast_fusion.1, f32[16,5,32,128]{3,2,1,0:T(8,128)S(1)} %constant_dynamic-slice_fusion.1), kind=kLoop, calls=%fused_computation.1 | loop fusion | flops 348160 | bytes 2785280 | tf_op jit(solution)/shard_map/concatenate | solution.py:201
  13.2 1.3 %collective-permute-start.4 = (f32[17,5,32,128]{3,2,1,0:T(8,128)}, f32[17,5,32,128]{3,2,1,0:T(8,128)S(1)}, u32[]{:S(2)}, u32[]{:S(2)}) collective-permute-start(f32[17,5,32,128]{3,2,1,0:T(8,128)} %pad_maximum_fusion.1), channel_id=1, source_target_pairs={{24,28},{20,16},{8,12},{4,0},{25,29},{21,17},{9,13},{5,1},{26,30},... | collective-permute-start | bytes 4177928 | tf_op jit(solution)/shard_map/ppermute | solution.py:216
  14.5 1.5 %fusion.4 = (f32[16,12,2,128]{3,2,1,0:T(2,128)S(1)}, f32[16,12,2,128]{3,2,1,0:T(2,128)S(1)}) fusion(f32[16,12,32,128]{3,2,1,0:T(8,128)} %refs_0_.1), kind=kLoop, calls=%fused_computation.24 | loop fusion | bytes 786432 | tf_op jit(solution)/shard_map/slice | solution.py:205
  16.0 0.8 pad_maximum_fusion.5
  16.8 3.1 %collective-permute-start.1 = (f32[17,12,2,128]{3,2,1,0:T(2,128)}, f32[17,12,2,128]{3,2,1,0:T(2,128)S(1)}, u32[]{:S(2)}, u32[]{:S(2)}) collective-permute-start(f32[17,12,2,128]{3,2,1,0:T(2,128)} %pad_maximum_fusion.5), channel_id=1, source_target_pairs={{0,1},{1,2},{2,3},{3,0},{4,5},{5,6},{6,7},{7,4},{8,9},{9,10},{10,1... | collective-permute-start | bytes 626696 | tf_op jit(solution)/shard_map/ppermute | solution.py:206
  19.8 0.8 pad_maximum_fusion.4
  20.6 2.0 %collective-permute-start = (f32[17,12,2,128]{3,2,1,0:T(2,128)}, f32[17,12,2,128]{3,2,1,0:T(2,128)S(1)}, u32[]{:S(2)}, u32[]{:S(2)}) collective-permute-start(f32[17,12,2,128]{3,2,1,0:T(2,128)} %pad_maximum_fusion.4), channel_id=1, source_target_pairs={{1,0},{2,1},{3,2},{0,3},{5,4},{6,5},{7,6},{4,7},{9,8},{10,9},{11,1... | collective-permute-start | bytes 626696 | tf_op jit(solution)/shard_map/ppermute | solution.py:205
  24.6 1.1 %constant_dynamic-slice_fusion = f32[16,2,32,128]{3,2,1,0:T(8,128)S(1)} fusion(f32[16,12,32,128]{3,2,1,0:T(8,128)} %refs_0_.1, s32[]{:T(128)S(6)} %select_n.21), kind=kLoop, calls=%fused_computation.18 | loop fusion | bytes 1048580 | tf_op jit(solution)/shard_map/dynamic_slice | solution.py:201
  25.7 0.8 dynamic-slice_bitcast_fusion.2
  26.5 3.6 %collective-permute-start.6 = (f32[17,2,32,128]{3,2,1,0:T(8,128)S(1)}, f32[17,2,32,128]{3,2,1,0:T(8,128)S(1)}, u32[]{:S(2)}, u32[]{:S(2)}) collective-permute-start(f32[17,2,32,128]{3,2,1,0:T(8,128)S(1)} %pad_maximum_fusion.3), channel_id=1, source_target_pairs={{28,0},{16,12},{12,16},{0,28},{29,1},{17,13},{13,17},{1,29},{30,2}... | collective-permute-start | bytes 1671176 | tf_op jit(solution)/shard_map/ppermute | solution.py:216
  30.2 0.0 collective-permute-done.1
  30.2 2.3 %collective-permute-done = f32[17,12,2,128]{3,2,1,0:T(2,128)S(1)} collective-permute-done((f32[17,12,2,128]{3,2,1,0:T(2,128)}, f32[17,12,2,128]{3,2,1,0:T(2,128)S(1)}, u32[]{:S(2)}, u32[]{:S(2)}) %collective-permute-start) | collective-permute-done | bytes 208928 | tf_op jit(solution)/shard_map/ppermute | solution.py:205
  32.5 3.0 %collective-permute-start.7 = (f32[17,2,4,128]{3,2,1,0:T(4,128)S(1)}, f32[17,2,4,128]{3,2,1,0:T(4,128)S(1)}, u32[]{:S(2)}, u32[]{:S(2)}) collective-permute-start(f32[17,2,4,128]{3,2,1,0:T(4,128)S(1)} %fusion.2), channel_id=1, source_target_pairs={{28,0},{16,12},{12,16},{0,28},{29,1},{17,13},{13,17},{1,29},{30,2}... | collective-permute-start | bytes 208904 | tf_op jit(solution)/shard_map/ppermute | solution.py:217
  35.5 0.1 fusion
  35.6 0.7 collective-permute-start.3
  36.3 0.1 fusion.1
  36.4 4.0 %collective-permute-done.7.refs_14_.refs_15_ = f32[17,2,4,128]{3,2,1,0:T(4,128)S(1)} collective-permute-done((f32[17,2,4,128]{3,2,1,0:T(4,128)S(1)}, f32[17,2,4,128]{3,2,1,0:T(4,128)S(1)}, u32[]{:S(2)}, u32[]{:S(2)}) %collective-permute-start.7) | collective-permute-done | bytes 69664 | tf_op jit(solution)/shard_map/ppermute | solution.py:217
  40.4 1.3 %collective-permute-start.5 = (f32[17,5,4,128]{3,2,1,0:T(4,128)S(1)}, f32[17,5,4,128]{3,2,1,0:T(4,128)S(1)}, u32[]{:S(2)}, u32[]{:S(2)}) collective-permute-start(f32[17,5,4,128]{3,2,1,0:T(4,128)S(1)} %fusion.1), channel_id=1, source_target_pairs={{24,28},{20,16},{8,12},{4,0},{25,29},{21,17},{9,13},{5,1},{26,30},... | collective-permute-start | bytes 522248 | tf_op jit(solution)/shard_map/ppermute | solution.py:217
  41.6 0.2 pad_maximum_fusion.2.refs_2_.refs_3_
  41.8 1.8 %collective-permute-done.5.refs_10_.refs_11_ = f32[17,5,4,128]{3,2,1,0:T(4,128)S(1)} collective-permute-done((f32[17,5,4,128]{3,2,1,0:T(4,128)S(1)}, f32[17,5,4,128]{3,2,1,0:T(4,128)S(1)}, u32[]{:S(2)}, u32[]{:S(2)}) %collective-permute-start.5) | collective-permute-done | bytes 174112 | tf_op jit(solution)/shard_map/ppermute | solution.py:217
  43.7 0.0 collective-permute-done.2.refs_4_.refs_5_
  43.7 22.3 %laplace.1 = (f32[16,15,32,128]{3,2,1,0:T(8,128)}, f32[16,128]{1,0:T(8,128)S(1)}) custom-call(s32[10]{0:T(128)S(1)} %fusion.3.table, f32[16,12,32,128]{3,2,1,0:T(8,128)} %refs_0_.1, s32[12,32,128]{2,1,0:T(8,128)S(1)} %copy-done, f32[17,12,4,128]{3,2,1,0:T(4,128)S(1)} %pad_maximum_fusion.2.refs_2_.refs_3_, ...), custom_call_target="tpu_custom_call" | custom-call | tf_op jit(solution)/shard_map/laplace/pallas_call | solution.py:236
  66.0 0.6 copy-done.1
  66.6 13.1 %gram_sum.1 = f32[2,16,128]{2,1,0:T(8,128)} custom-call(f32[16,128]{1,0:T(8,128)} %copy-done.1), custom_call_target="tpu_custom_call" | custom-call | tf_op jit(solution)/shard_map/gram_sum/pallas_call | solution.py:265
  79.7 1.3 %copy.6 = f32[2,16,16]{2,1,0:T(8,128)} copy(f32[2,16,16]{2,1,0:T(8,128)} %bitcast.14) | data formatting | bytes 4096
  (13 shorter events, 0.1 us)
Async XLA Ops:
  4.2 6.2 %copy-start.2 = (f32[12,32,128]{2,1,0:T(8,128)}, f32[12,32,128]{2,1,0:T(8,128)S(1)}, u32[]{:S(2)}) copy-start(f32[12,32,128]{2,1,0:T(8,128)S(1)} %get-tuple-element.8) | copy-start | bytes 589828
  7.9 35.8 %collective-permute-start.2 = (f32[17,6,32,128]{3,2,1,0:T(8,128)}, f32[17,6,32,128]{3,2,1,0:T(8,128)S(1)}, u32[]{:S(2)}, u32[]{:S(2)}) collective-permute-start(f32[17,6,32,128]{3,2,1,0:T(8,128)} %pad_maximum_fusion), channel_id=1, source_target_pairs={{24,20},{20,24},{8,4},{4,8},{25,21},{21,25},{9,5},{5,9},{26,22},{2... | collective-permute-start | bytes 5013512 | tf_op jit(solution)/shard_map/ppermute | solution.py:216
  13.2 30.5 %collective-permute-start.4 = (f32[17,5,32,128]{3,2,1,0:T(8,128)}, f32[17,5,32,128]{3,2,1,0:T(8,128)S(1)}, u32[]{:S(2)}, u32[]{:S(2)}) collective-permute-start(f32[17,5,32,128]{3,2,1,0:T(8,128)} %pad_maximum_fusion.1), channel_id=1, source_target_pairs={{24,28},{20,16},{8,12},{4,0},{25,29},{21,17},{9,13},{5,1},{26,30},... | collective-permute-start | bytes 4177928 | tf_op jit(solution)/shard_map/ppermute | solution.py:216
  16.8 13.4 %collective-permute-start.1 = (f32[17,12,2,128]{3,2,1,0:T(2,128)}, f32[17,12,2,128]{3,2,1,0:T(2,128)S(1)}, u32[]{:S(2)}, u32[]{:S(2)}) collective-permute-start(f32[17,12,2,128]{3,2,1,0:T(2,128)} %pad_maximum_fusion.5), channel_id=1, source_target_pairs={{0,1},{1,2},{2,3},{3,0},{4,5},{5,6},{6,7},{7,4},{8,9},{9,10},{10,1... | collective-permute-start | bytes 626696 | tf_op jit(solution)/shard_map/ppermute | solution.py:206
  20.6 11.8 %collective-permute-start = (f32[17,12,2,128]{3,2,1,0:T(2,128)}, f32[17,12,2,128]{3,2,1,0:T(2,128)S(1)}, u32[]{:S(2)}, u32[]{:S(2)}) collective-permute-start(f32[17,12,2,128]{3,2,1,0:T(2,128)} %pad_maximum_fusion.4), channel_id=1, source_target_pairs={{1,0},{2,1},{3,2},{0,3},{5,4},{6,5},{7,6},{4,7},{9,8},{10,9},{11,1... | collective-permute-start | bytes 626696 | tf_op jit(solution)/shard_map/ppermute | solution.py:205
  26.5 17.2 %copy-start = (s32[12,32,128]{2,1,0:T(8,128)S(1)}, s32[12,32,128]{2,1,0:T(8,128)}, u32[]{:S(2)}) copy-start(s32[12,32,128]{2,1,0:T(8,128)} %refs_1_.1) | copy-start | bytes 589828
  26.5 17.1 %collective-permute-start.6 = (f32[17,2,32,128]{3,2,1,0:T(8,128)S(1)}, f32[17,2,32,128]{3,2,1,0:T(8,128)S(1)}, u32[]{:S(2)}, u32[]{:S(2)}) collective-permute-start(f32[17,2,32,128]{3,2,1,0:T(8,128)S(1)} %pad_maximum_fusion.3), channel_id=1, source_target_pairs={{28,0},{16,12},{12,16},{0,28},{29,1},{17,13},{13,17},{1,29},{30,2}... | collective-permute-start | bytes 1671176 | tf_op jit(solution)/shard_map/ppermute | solution.py:216
  32.5 7.8 %collective-permute-start.7 = (f32[17,2,4,128]{3,2,1,0:T(4,128)S(1)}, f32[17,2,4,128]{3,2,1,0:T(4,128)S(1)}, u32[]{:S(2)}, u32[]{:S(2)}) collective-permute-start(f32[17,2,4,128]{3,2,1,0:T(4,128)S(1)} %fusion.2), channel_id=1, source_target_pairs={{28,0},{16,12},{12,16},{0,28},{29,1},{17,13},{13,17},{1,29},{30,2}... | collective-permute-start | bytes 208904 | tf_op jit(solution)/shard_map/ppermute | solution.py:217
  35.6 8.1 %collective-permute-start.3 = (f32[17,6,4,128]{3,2,1,0:T(4,128)S(1)}, f32[17,6,4,128]{3,2,1,0:T(4,128)S(1)}, u32[]{:S(2)}, u32[]{:S(2)}) collective-permute-start(f32[17,6,4,128]{3,2,1,0:T(4,128)S(1)} %fusion), channel_id=1, source_target_pairs={{24,20},{20,24},{8,4},{4,8},{25,21},{21,25},{9,5},{5,9},{26,22},{2... | collective-permute-start | bytes 626696 | tf_op jit(solution)/shard_map/ppermute | solution.py:217
  40.4 3.3 %collective-permute-start.5 = (f32[17,5,4,128]{3,2,1,0:T(4,128)S(1)}, f32[17,5,4,128]{3,2,1,0:T(4,128)S(1)}, u32[]{:S(2)}, u32[]{:S(2)}) collective-permute-start(f32[17,5,4,128]{3,2,1,0:T(4,128)S(1)} %fusion.1), channel_id=1, source_target_pairs={{24,28},{20,16},{8,12},{4,0},{25,29},{21,17},{9,13},{5,1},{26,30},... | collective-permute-start | bytes 522248 | tf_op jit(solution)/shard_map/ppermute | solution.py:217
  66.0 0.6 copy-start.1
